TPU v7x, 1024 devices: a whole 4x4x32 slice. The times are simulated.
1024 devices in a mesh: ctx: 128 (over z, x), tp: 8 (over y, core).
Axes of the slice: x: 4, y: 4, z: 32, core: 2. Of those that a mesh axis runs over, the one named last changes fastest.
Arguments:
- queries: bfloat16 [32768, 8192], P(('ctx', 'tp')), may hold values from -6 to 6
- keys: bfloat16 [32768, 1024], P(('ctx', 'tp')), may hold values from -6 to 6
- values: bfloat16 [32768, 1024], P(('ctx', 'tp')), may hold values from -6 to 6
- doc_starts: int32 [77], replicated, may hold values from 0 to 32768, as said below
Outputs:
- attended: bfloat16 [32768, 8192], P(('ctx', 'tp'))
Inputs may be any that keep to these rules, and one draw needn't show every extreme that they name: `doc_starts`: nondecreasing and starting with 0; consecutive entries differ by at most 1792, and some pair of consecutive entries below 32768 differs by exactly 1792; the last document ends at 32768, and entries equal to 32768 stand for empty documents.
All inputs are finite; a program needn't handle non-finite values.
Results may differ from a plain program's by a relative error of at most 0.004.
Values may be sent and summed in bfloat16 or wider, within the bound.
No kernel may reach another device: no remote copies, remote signals or barrier semaphores. Data moves between devices by JAX's collectives and lax.ppermute only.
A program may use at most 32 MiB of HBM per device.

v0:
```python
import jax
import jax.numpy as jnp
from jax import lax
from jax.sharding import PartitionSpec as P

QUERY_HEAD_COUNT = 64
KEY_VALUE_HEADS = 8
HEAD_WIDTH = 128


def passed_along(block, axis, distance):
    devices = range(lax.axis_size(axis))
    route = [(i - distance, i) for i in devices if i - distance in devices]
    return lax.ppermute(block, axis, route)


def doc_begin(positions, doc_starts):
    found = jnp.where(doc_starts[None, :] <= positions[:, None], doc_starts[None, :], 0)
    return jnp.max(found, axis=1)


def body(queries, keys, values, doc_starts):
    query_matrix, key_matrix, value_matrix = (
        lax.all_to_all(queries, "tp", split_axis=1, concat_axis=0, tiled=True),
        lax.all_to_all(keys, "tp", split_axis=1, concat_axis=0, tiled=True),
        lax.all_to_all(values, "tp", split_axis=1, concat_axis=0, tiled=True),
    )
    rows_per_block = query_matrix.shape[0]
    kv_local = key_matrix.shape[1] // HEAD_WIDTH
    query_groups = QUERY_HEAD_COUNT // KEY_VALUE_HEADS
    scale = HEAD_WIDTH ** (-0.5)
    reach_blocks = min(8, lax.axis_size("ctx") // 2)
    ctx_index = lax.axis_index("ctx")
    query_pos = ctx_index * rows_per_block + jnp.arange(rows_per_block, dtype=jnp.int32)
    begins = doc_begin(query_pos, doc_starts)
    query_heads = query_matrix.reshape(rows_per_block, kv_local, query_groups, HEAD_WIDTH)
    initial = (
        jnp.full((kv_local, query_groups, rows_per_block), -1e30, jnp.float32),
        jnp.zeros((kv_local, query_groups, rows_per_block), jnp.float32),
        jnp.zeros((kv_local, query_groups, rows_per_block, HEAD_WIDTH), jnp.float32),
    )

    def attend(state, pair, key_start):
        running_max, running_sum, accum = state
        key_tile = pair[0].reshape(rows_per_block, kv_local, HEAD_WIDTH)
        value_tile = pair[1].reshape(rows_per_block, kv_local, HEAD_WIDTH)
        scores = (
            jnp.einsum("qkgd,pkd->kgqp", query_heads, key_tile, preferred_element_type=jnp.float32)
            * scale
        )
        key_pos = key_start + jnp.arange(rows_per_block, dtype=jnp.int32)
        visible = (key_pos[None, :] <= query_pos[:, None]) & (key_pos[None, :] >= begins[:, None])
        scores = jnp.where(visible, scores, -1e30)
        new_max = jnp.maximum(running_max, jnp.max(scores, axis=-1))
        probs = jnp.where(visible, jnp.exp(scores - new_max[..., None]), 0.0)
        factor = jnp.exp(running_max - new_max)
        new_sum = running_sum * factor + jnp.sum(probs, axis=-1)
        update = jnp.einsum(
            "kgqp,pkd->kgqd",
            probs.astype(jnp.bfloat16),
            value_tile,
            preferred_element_type=jnp.float32,
        )
        return (new_max, new_sum, accum * factor[..., None] + update)

    paired = jnp.stack((key_matrix, value_matrix))
    visible_span = paired
    for level in range(reach_blocks.bit_length() - 1):
        farther = passed_along(visible_span, "ctx", 1 << level)
        visible_span = jnp.concatenate([visible_span, farther], axis=1)

    def visit(step, current):
        piece = lax.dynamic_slice_in_dim(
            visible_span, (step * rows_per_block).astype(jnp.int32), rows_per_block, 1
        )
        return attend(current, piece, (ctx_index - step) * rows_per_block)

    state = lax.fori_loop(0, reach_blocks, visit, initial)
    result = state[2] / state[1][..., None]
    result = (
        jnp.transpose(result, (2, 0, 1, 3))
        .reshape(rows_per_block, kv_local * query_groups * HEAD_WIDTH)
        .astype(jnp.bfloat16)
    )
    return lax.all_to_all(result, "tp", split_axis=0, concat_axis=1, tiled=True)


def solution(mesh):
    in_specs = (P(("ctx", "tp"), None), P(("ctx", "tp"), None), P(("ctx", "tp"), None), P())
    out_specs = P(("ctx", "tp"), None)
    return jax.shard_map(body, mesh=mesh, in_specs=in_specs, out_specs=out_specs, check_vma=False)
```

profile of v0, /device:TPU:352, one launch (start us, length us, event | category | flops | bytes accessed | tf_op | source)
XLA Modules:
  0.0 120.4 jit_solution(7199657623059419430)
XLA Ops:
  1.5 4.5 %all-to-all-start = ((bf16[32,8,128]{2,0,1:T(8,128)(2,1)}), bf16[32,8,128]{2,0,1:T(8,128)(2,1)S(1)}, u32[]{:S(2)}, u32[]{:S(2)}) async-start(bf16[32,8,128]{2,0,1:T(8,128)(2,1)} %copy_bitcast_fusion.2), calls=%async_computation | async-start | bytes 131072 | tf_op jit(solution)/shard_map/all_to_all | solution.py:25
  6.8 4.8 %all-to-all-done = bf16[32,8,128]{2,0,1:T(8,128)(2,1)S(1)} async-done(((bf16[32,8,128]{2,0,1:T(8,128)(2,1)}), bf16[32,8,128]{2,0,1:T(8,128)(2,1)S(1)}, u32[]{:S(2)}, u32[]{:S(2)}) %all-to-all-start) | async-done | bytes 65568 | tf_op jit(solution)/shard_map/all_to_all | solution.py:25
  11.6 8.0 %all_to_all.64 = bf16[32,8,128]{2,0,1:T(8,128)(2,1)S(1)} all-to-all(bf16[32,8,128]{2,0,1:T(8,128)(2,1)S(1)} %copy_bitcast_fusion.1), channel_id=1, replica_groups=mesh['ctx'=128,'tp'=8] {'tp'}, dimensions={1} | all-to-all | bytes 131072 | tf_op jit(solution)/shard_map/all_to_all | solution.py:26
  19.6 3.4 %collective-permute-start = (bf16[2,256,128]{2,1,0:T(8,128)(2,1)S(1)}, bf16[2,256,128]{2,1,0:T(8,128)(2,1)S(1)}, u32[]{:S(2)}, u32[]{:S(2)}) collective-permute-start(bf16[2,256,128]{2,1,0:T(8,128)(2,1)S(1)} %pad_maximum_fusion.3), channel_id=1, source_target_pairs={{0,8},{8,16},{16,24},{24,32},{32,40},{40,48},{48,56},{56,64},{64,7... | collective-permute-start | bytes 393224 | tf_op jit(solution)/shard_map/ppermute | solution.py:14
  23.0 5.7 %collective-permute-done = bf16[2,256,128]{2,1,0:T(8,128)(2,1)S(1)} collective-permute-done((bf16[2,256,128]{2,1,0:T(8,128)(2,1)S(1)}, bf16[2,256,128]{2,1,0:T(8,128)(2,1)S(1)}, u32[]{:S(2)}, u32[]{:S(2)}) %collective-permute-start) | collective-permute-done | bytes 131104 | tf_op jit(solution)/shard_map/ppermute | solution.py:14
  28.7 2.8 %collective-permute-start.1 = (bf16[2,512,128]{2,1,0:T(8,128)(2,1)S(1)}, bf16[2,512,128]{2,1,0:T(8,128)(2,1)S(1)}, u32[]{:S(2)}, u32[]{:S(2)}) collective-permute-start(bf16[2,512,128]{2,1,0:T(8,128)(2,1)S(1)} %pad_maximum_fusion.2), channel_id=1, source_target_pairs={{0,16},{8,24},{16,32},{24,40},{32,48},{40,56},{48,64},{56,72},{64,... | collective-permute-start | bytes 786440 | tf_op jit(solution)/shard_map/ppermute | solution.py:14
  31.6 8.6 %collective-permute-done.1 = bf16[2,512,128]{2,1,0:T(8,128)(2,1)S(1)} collective-permute-done((bf16[2,512,128]{2,1,0:T(8,128)(2,1)S(1)}, bf16[2,512,128]{2,1,0:T(8,128)(2,1)S(1)}, u32[]{:S(2)}, u32[]{:S(2)}) %collective-permute-start.1) | collective-permute-done | bytes 262176 | tf_op jit(solution)/shard_map/ppermute | solution.py:14
  40.2 7.5 %collective-permute-start.2 = (bf16[2,1024,128]{2,1,0:T(8,128)(2,1)S(1)}, bf16[2,1024,128]{2,1,0:T(8,128)(2,1)S(1)}, u32[]{:S(2)}, u32[]{:S(2)}) collective-permute-start(bf16[2,1024,128]{2,1,0:T(8,128)(2,1)S(1)} %pad_maximum_fusion.1), channel_id=1, source_target_pairs={{0,32},{8,40},{16,48},{24,56},{32,64},{40,72},{48,80},{56,88},{64,... | collective-permute-start | bytes 1572872 | tf_op jit(solution)/shard_map/ppermute | solution.py:14
  48.5 3.5 %all-to-all-start.2 = ((bf16[32,8,1024]{2,0,1:T(8,128)(2,1)}), bf16[32,8,1024]{2,0,1:T(8,128)(2,1)S(1)}, u32[]{:S(2)}, u32[]{:S(2)}) async-start(bf16[32,8,1024]{2,0,1:T(8,128)(2,1)} %bitcast.80), calls=%async_computation.2 | async-start | bytes 1048576 | tf_op jit(solution)/shard_map/all_to_all | solution.py:24
  52.1 10.1 %all-to-all-done.2 = bf16[32,8,1024]{2,0,1:T(8,128)(2,1)S(1)} async-done(((bf16[32,8,1024]{2,0,1:T(8,128)(2,1)}), bf16[32,8,1024]{2,0,1:T(8,128)(2,1)S(1)}, u32[]{:S(2)}, u32[]{:S(2)}) %all-to-all-start.2) | async-done | bytes 524320 | tf_op jit(solution)/shard_map/all_to_all | solution.py:24
  63.4 41.2 %while.18 = (s32[]{:T(128)}, f32[1,8,256]{2,1,0:T(8,128)S(1)}, f32[1,8,256]{2,1,0:T(8,128)S(1)}, f32[1,8,256,128]{3,2,1,0:T(8,128)}, s32[]{:T(128)}, /*index=5*/...) while((s32[]{:T(128)}, f32[1,8,256]{2,1,0:T(8,128)S(1)}, ...), condition=%wide.region_4.5_spmd.clone, body=%wide.region_1.4_spmd.clone.sunk | while | flops 276247040 | bytes 9442551 | solution.py:78
  63.6 1.3 %fusion.30 = (f32[8,256]{1,0:T(8,128)S(1)}, f32[256,256,8]{1,0,2:T(8,128)S(1)}) fusion(pred[256,256]{0,1:T(8,128)(4,1)S(1)} %compare_and_fusion.2, bf16[256,1,8,128]{3,0,2,1:T(8,128)(2,1)S(1)} %get-tuple-element.348, bf16[2,2048,128]{2,1,0:T(8,128)(2,1)} %get-tuple-element.347, s32[]{:T(128)S(6)} %select_n.62), kind=kOutput, calls=%fused_computation.3.clone.1 | convolution fusion | flops 135788544 | bytes 2760708 | tf_op jit(solution)/shard_map/while/body/eval_jaxpr/qkgd,pkd->kgqp/dot_general | solution.py:48
  64.9 2.7 %fusion.33 = f32[1,8,256,128]{3,2,1,0:T(8,128)} fusion(f32[256,256,8]{1,0,2:T(8,128)S(1)} %get-tuple-element.311, f32[1,8,256,128]{3,2,1,0:T(8,128)} %get-tuple-element.330, f32[8,256]{1,0:T(8,128)S(1)} %bitcast.103, pred[256,256]{0,1:T(8,128)(4,1)S(1)} %compare_and_fusion.2, f32[8,256]{1,0:T(8,128)S(1)} %get-tuple-element.312, pred[]{:T(512)S(6)} %compare.3, ...), kind=kOutput, calls=%fused_computation.7.clone.1 | convolution fusion | flops 137625600 | bytes 4341769 | tf_op jit(solution)/shard_map/while/body/eval_jaxpr/kgqp,pkd->kgqd/dot_general | solution.py:58
  69.7 3.2 %fusion.33 = f32[1,8,256,128]{3,2,1,0:T(8,128)} fusion(f32[256,256,8]{1,0,2:T(8,128)S(1)} %get-tuple-element.311, f32[1,8,256,128]{3,2,1,0:T(8,128)} %get-tuple-element.330, f32[8,256]{1,0:T(8,128)S(1)} %bitcast.103, pred[256,256]{0,1:T(8,128)(4,1)S(1)} %compare_and_fusion.2, f32[8,256]{1,0:T(8,128)S(1)} %get-tuple-element.312, pred[]{:T(512)S(6)} %compare.3, ...), kind=kOutput, calls=%fused_computation.7.clone.1 | convolution fusion | flops 137625600 | bytes 4341769 | tf_op jit(solution)/shard_map/while/body/eval_jaxpr/kgqp,pkd->kgqd/dot_general | solution.py:58
  73.6 1.3 %fusion.30 = (f32[8,256]{1,0:T(8,128)S(1)}, f32[256,256,8]{1,0,2:T(8,128)S(1)}) fusion(pred[256,256]{0,1:T(8,128)(4,1)S(1)} %compare_and_fusion.2, bf16[256,1,8,128]{3,0,2,1:T(8,128)(2,1)S(1)} %get-tuple-element.348, bf16[2,2048,128]{2,1,0:T(8,128)(2,1)} %get-tuple-element.347, s32[]{:T(128)S(6)} %select_n.62), kind=kOutput, calls=%fused_computation.3.clone.1 | convolution fusion | flops 135788544 | bytes 2760708 | tf_op jit(solution)/shard_map/while/body/eval_jaxpr/qkgd,pkd->kgqp/dot_general | solution.py:48
  74.9 3.2 %fusion.33 = f32[1,8,256,128]{3,2,1,0:T(8,128)} fusion(f32[256,256,8]{1,0,2:T(8,128)S(1)} %get-tuple-element.311, f32[1,8,256,128]{3,2,1,0:T(8,128)} %get-tuple-element.330, f32[8,256]{1,0:T(8,128)S(1)} %bitcast.103, pred[256,256]{0,1:T(8,128)(4,1)S(1)} %compare_and_fusion.2, f32[8,256]{1,0:T(8,128)S(1)} %get-tuple-element.312, pred[]{:T(512)S(6)} %compare.3, ...), kind=kOutput, calls=%fused_computation.7.clone.1 | convolution fusion | flops 137625600 | bytes 4341769 | tf_op jit(solution)/shard_map/while/body/eval_jaxpr/kgqp,pkd->kgqd/dot_general | solution.py:58
  80.1 3.2 %fusion.33 = f32[1,8,256,128]{3,2,1,0:T(8,128)} fusion(f32[256,256,8]{1,0,2:T(8,128)S(1)} %get-tuple-element.311, f32[1,8,256,128]{3,2,1,0:T(8,128)} %get-tuple-element.330, f32[8,256]{1,0:T(8,128)S(1)} %bitcast.103, pred[256,256]{0,1:T(8,128)(4,1)S(1)} %compare_and_fusion.2, f32[8,256]{1,0:T(8,128)S(1)} %get-tuple-element.312, pred[]{:T(512)S(6)} %compare.3, ...), kind=kOutput, calls=%fused_computation.7.clone.1 | convolution fusion | flops 137625600 | bytes 4341769 | tf_op jit(solution)/shard_map/while/body/eval_jaxpr/kgqp,pkd->kgqd/dot_general | solution.py:58
  84.0 1.3 %fusion.30 = (f32[8,256]{1,0:T(8,128)S(1)}, f32[256,256,8]{1,0,2:T(8,128)S(1)}) fusion(pred[256,256]{0,1:T(8,128)(4,1)S(1)} %compare_and_fusion.2, bf16[256,1,8,128]{3,0,2,1:T(8,128)(2,1)S(1)} %get-tuple-element.348, bf16[2,2048,128]{2,1,0:T(8,128)(2,1)} %get-tuple-element.347, s32[]{:T(128)S(6)} %select_n.62), kind=kOutput, calls=%fused_computation.3.clone.1 | convolution fusion | flops 135788544 | bytes 2760708 | tf_op jit(solution)/shard_map/while/body/eval_jaxpr/qkgd,pkd->kgqp/dot_general | solution.py:48
  85.3 3.2 %fusion.33 = f32[1,8,256,128]{3,2,1,0:T(8,128)} fusion(f32[256,256,8]{1,0,2:T(8,128)S(1)} %get-tuple-element.311, f32[1,8,256,128]{3,2,1,0:T(8,128)} %get-tuple-element.330, f32[8,256]{1,0:T(8,128)S(1)} %bitcast.103, pred[256,256]{0,1:T(8,128)(4,1)S(1)} %compare_and_fusion.2, f32[8,256]{1,0:T(8,128)S(1)} %get-tuple-element.312, pred[]{:T(512)S(6)} %compare.3, ...), kind=kOutput, calls=%fused_computation.7.clone.1 | convolution fusion | flops 137625600 | bytes 4341769 | tf_op jit(solution)/shard_map/while/body/eval_jaxpr/kgqp,pkd->kgqd/dot_general | solution.py:58
  90.5 3.2 %fusion.33 = f32[1,8,256,128]{3,2,1,0:T(8,128)} fusion(f32[256,256,8]{1,0,2:T(8,128)S(1)} %get-tuple-element.311, f32[1,8,256,128]{3,2,1,0:T(8,128)} %get-tuple-element.330, f32[8,256]{1,0:T(8,128)S(1)} %bitcast.103, pred[256,256]{0,1:T(8,128)(4,1)S(1)} %compare_and_fusion.2, f32[8,256]{1,0:T(8,128)S(1)} %get-tuple-element.312, pred[]{:T(512)S(6)} %compare.3, ...), kind=kOutput, calls=%fused_computation.7.clone.1 | convolution fusion | flops 137625600 | bytes 4341769 | tf_op jit(solution)/shard_map/while/body/eval_jaxpr/kgqp,pkd->kgqd/dot_general | solution.py:58
  95.7 3.2 %fusion.33 = f32[1,8,256,128]{3,2,1,0:T(8,128)} fusion(f32[256,256,8]{1,0,2:T(8,128)S(1)} %get-tuple-element.311, f32[1,8,256,128]{3,2,1,0:T(8,128)} %get-tuple-element.330, f32[8,256]{1,0:T(8,128)S(1)} %bitcast.103, pred[256,256]{0,1:T(8,128)(4,1)S(1)} %compare_and_fusion.2, f32[8,256]{1,0:T(8,128)S(1)} %get-tuple-element.312, pred[]{:T(512)S(6)} %compare.3, ...), kind=kOutput, calls=%fused_computation.7.clone.1 | convolution fusion | flops 137625600 | bytes 4341769 | tf_op jit(solution)/shard_map/while/body/eval_jaxpr/kgqp,pkd->kgqd/dot_general | solution.py:58
  100.9 3.2 %fusion.33 = f32[1,8,256,128]{3,2,1,0:T(8,128)} fusion(f32[256,256,8]{1,0,2:T(8,128)S(1)} %get-tuple-element.311, f32[1,8,256,128]{3,2,1,0:T(8,128)} %get-tuple-element.330, f32[8,256]{1,0:T(8,128)S(1)} %bitcast.103, pred[256,256]{0,1:T(8,128)(4,1)S(1)} %compare_and_fusion.2, f32[8,256]{1,0:T(8,128)S(1)} %get-tuple-element.312, pred[]{:T(512)S(6)} %compare.3, ...), kind=kOutput, calls=%fused_computation.7.clone.1 | convolution fusion | flops 137625600 | bytes 4341769 | tf_op jit(solution)/shard_map/while/body/eval_jaxpr/kgqp,pkd->kgqd/dot_general | solution.py:58
  104.6 1.6 %fusion.21 = bf16[256,1,8,128]{3,0,2,1:T(8,128)(2,1)S(1)} fusion(f32[1,8,256,128]{3,2,1,0:T(8,128)} %get-tuple-element.160, f32[8,256]{1,0:T(8,128)S(1)} %bitcast.117), kind=kLoop, calls=%fused_computation.36 | loop fusion | flops 524288 | bytes 1581056 | tf_op jit(solution)/shard_map/convert_element_type | solution.py:83
  106.8 12.8 %all_to_all.65 = bf16[8,32,1024]{2,1,0:T(8,128)(2,1)S(1)} all-to-all(bf16[8,32,1024]{2,1,0:T(8,128)(2,1)S(1)} %convert_element_type.19), channel_id=1, replica_groups=mesh['ctx'=128,'tp'=8] {'tp'}, dimensions={0} | all-to-all | bytes 1048576 | tf_op jit(solution)/shard_map/all_to_all | solution.py:85
  (77 shorter events, 17.8 us)
Async XLA Ops:
  0.0 0.8 copy-start
  0.0 47.6 %copy-start.1 = (bf16[32,8192]{1,0:T(8,128)(2,1)S(1)}, bf16[32,8192]{1,0:T(8,128)(2,1)}, u32[]{:S(2)}) copy-start(bf16[32,8192]{1,0:T(8,128)(2,1)} %param.6) | copy-start | bytes 1572868
  1.5 10.1 %all-to-all-start = ((bf16[32,8,128]{2,0,1:T(8,128)(2,1)}), bf16[32,8,128]{2,0,1:T(8,128)(2,1)S(1)}, u32[]{:S(2)}, u32[]{:S(2)}) async-start(bf16[32,8,128]{2,0,1:T(8,128)(2,1)} %copy_bitcast_fusion.2), calls=%async_computation | async-start | bytes 131072 | tf_op jit(solution)/shard_map/all_to_all | solution.py:25
  6.0 46.1 %copy-start.2 = (s32[77]{0:T(128)S(1)}, s32[77]{0:T(128)}, u32[]{:S(2)}) copy-start(s32[77]{0:T(128)} %param.9) | copy-start | bytes 928
  19.6 9.1 %collective-permute-start = (bf16[2,256,128]{2,1,0:T(8,128)(2,1)S(1)}, bf16[2,256,128]{2,1,0:T(8,128)(2,1)S(1)}, u32[]{:S(2)}, u32[]{:S(2)}) collective-permute-start(bf16[2,256,128]{2,1,0:T(8,128)(2,1)S(1)} %pad_maximum_fusion.3), channel_id=1, source_target_pairs={{0,8},{8,16},{16,24},{24,32},{32,40},{40,48},{48,56},{56,64},{64,7... | collective-permute-start | bytes 393224 | tf_op jit(solution)/shard_map/ppermute | solution.py:14
  28.7 11.4 %collective-permute-start.1 = (bf16[2,512,128]{2,1,0:T(8,128)(2,1)S(1)}, bf16[2,512,128]{2,1,0:T(8,128)(2,1)S(1)}, u32[]{:S(2)}, u32[]{:S(2)}) collective-permute-start(bf16[2,512,128]{2,1,0:T(8,128)(2,1)S(1)} %pad_maximum_fusion.2), channel_id=1, source_target_pairs={{0,16},{8,24},{16,32},{24,40},{32,48},{40,56},{48,64},{56,72},{64,... | collective-permute-start | bytes 786440 | tf_op jit(solution)/shard_map/ppermute | solution.py:14
  40.2 22.2 %collective-permute-start.2 = (bf16[2,1024,128]{2,1,0:T(8,128)(2,1)S(1)}, bf16[2,1024,128]{2,1,0:T(8,128)(2,1)S(1)}, u32[]{:S(2)}, u32[]{:S(2)}) collective-permute-start(bf16[2,1024,128]{2,1,0:T(8,128)(2,1)S(1)} %pad_maximum_fusion.1), channel_id=1, source_target_pairs={{0,32},{8,40},{16,48},{24,56},{32,64},{40,72},{48,80},{56,88},{64,... | collective-permute-start | bytes 1572872 | tf_op jit(solution)/shard_map/ppermute | solution.py:14
  48.5 13.7 %all-to-all-start.2 = ((bf16[32,8,1024]{2,0,1:T(8,128)(2,1)}), bf16[32,8,1024]{2,0,1:T(8,128)(2,1)S(1)}, u32[]{:S(2)}, u32[]{:S(2)}) async-start(bf16[32,8,1024]{2,0,1:T(8,128)(2,1)} %bitcast.80), calls=%async_computation.2 | async-start | bytes 1048576 | tf_op jit(solution)/shard_map/all_to_all | solution.py:24
where the time goes:
time: 121 us; the launch traced here: 120 us
  matrix products  35.3 us (29%)
  waiting for transfers between devices  29.1 us (24%)
  starting transfers between devices  21.6 us (18%)
  blocking collectives  20.8 us (17%)
  other arithmetic  8.05 us (7%)
  local copies, waits for them, and re-layouts  4.77 us (4%)
    dot_general x8, matrix products, attend(): jnp.einsum('kgqp,pkd->kgqd', probs.astype(jnp.bfloat16), value_tile, pref...  24.8 us
    ppermute x3, waiting for transfers between devices, passed_along(): return lax.ppermute(block, axis, route)  14.3 us
    ppermute x3, starting transfers between devices, passed_along(): return lax.ppermute(block, axis, route)  13.7 us
    all_to_all x1, blocking collectives, body(): return lax.all_to_all(result, 'tp', split_axis=0, concat_axis=1, tiled=True)  12.8 us
    dot_general x8, matrix products, attend(): jnp.einsum('qkgd,pkd->kgqp', query_heads, key_tile, preferred_element_typ...  10.5 us
    all_to_all x1, waiting for transfers between devices, body(): lax.all_to_all(queries, 'tp', split_axis=1, concat_axis=0, tiled=True)  10.1 us
    all_to_all x1, blocking collectives, body(): lax.all_to_all(values, 'tp', split_axis=1, concat_axis=0, tiled=True)  7.99 us
    all_to_all x1, waiting for transfers between devices, body(): lax.all_to_all(keys, 'tp', split_axis=1, concat_axis=0, tiled=True)  4.75 us
  transfers between devices with their start and end apart: 5, of which 4 were waited for; matrix products, arithmetic and copies ran while one was open for 2% of the time, Pallas kernels for 0%

commit v1 on v0

v1 whole, which is shorter than its diff:
```python
import jax
import jax.numpy as jnp
from jax import lax
from jax.experimental import pallas as pl
from jax.experimental.pallas import tpu as pltpu
from jax.sharding import Mesh, PartitionSpec as P


QUERY_HEAD_COUNT = 64
KEY_VALUE_HEADS = 8
HEAD_WIDTH = 128
GROUP = QUERY_HEAD_COUNT // KEY_VALUE_HEADS
ROW = 4
REACH = 8
HIDDEN = -1e30
EXP2_SCALE = HEAD_WIDTH ** (-0.5) * 1.4426950408889634
NT = (((1,), (1,)), ((), ()))


def doc_begin(positions, doc_starts):
    found = jnp.where(doc_starts[None, :] <= positions[:, None], doc_starts[None, :], 0)
    return jnp.max(found, axis=1)


def in_hbm(*arrays):
    return tuple(pltpu.with_memory_space_constraint(a, pltpu.HBM) for a in arrays)


def join_kernel(key_ref, value_ref, pair_ref, sem):
    tokens = key_ref.shape[0]
    copies = [
        pltpu.make_async_copy(key_ref, pair_ref.at[:tokens], sem.at[0]),
        pltpu.make_async_copy(value_ref, pair_ref.at[tokens:], sem.at[1]),
    ]
    for copy in copies:
        copy.start()
    for copy in copies:
        copy.wait()


def join(keys, values):
    anywhere, vmem = pl.BlockSpec(memory_space=pl.ANY), pl.BlockSpec(memory_space=pltpu.VMEM)
    return pl.pallas_call(
        join_kernel,
        out_shape=jax.ShapeDtypeStruct((2 * keys.shape[0], keys.shape[1]), keys.dtype),
        in_specs=[anywhere, anywhere],
        out_specs=vmem,
        scratch_shapes=[pltpu.SemaphoreType.DMA((2,))],
        compiler_params=pltpu.CompilerParams(vmem_limit_bytes=2 * 2**20),
        name="join",
    )(*in_hbm(keys, values))


def halve_kernel(query_ref, kept_ref, given_ref, sem):
    core = lax.axis_index("core")
    chips, _, width = kept_ref.shape
    copies = []
    for y in range(chips):
        for part, (into, owner) in enumerate(((kept_ref, core), (given_ref, 1 - core))):
            start = pl.multiple_of((2 * y + owner) * width, width)
            source = query_ref.at[:, pl.ds(start, width)]
            copies.append(pltpu.make_async_copy(source, into.at[y], sem.at[part, y]))
    for copy in copies:
        copy.start()
    for copy in copies:
        copy.wait()


def halve(queries, chips):
    anywhere, vmem = pl.BlockSpec(memory_space=pl.ANY), pl.BlockSpec(memory_space=pltpu.VMEM)
    half = jax.ShapeDtypeStruct((chips, queries.shape[0], GROUP * HEAD_WIDTH), queries.dtype)
    return pl.pallas_call(
        halve_kernel,
        out_shape=(half, half),
        in_specs=[anywhere],
        out_specs=(vmem, vmem),
        scratch_shapes=[pltpu.SemaphoreType.DMA((2, chips))],
        compiler_params=pltpu.CompilerParams(vmem_limit_bytes=4 * 2**20),
        name="halve",
    )(*in_hbm(queries))


def turn_kernel(kept_ref, other_ref, *out_refs):
    core, y = lax.axis_index("core"), lax.axis_index("y")
    chips, tokens, _ = kept_ref.shape
    for distance, out_ref in enumerate(out_refs):
        to = (y + distance) % chips
        out_ref[pl.ds(pl.multiple_of(core * tokens, tokens), tokens)] = kept_ref[to]
        out_ref[pl.ds(pl.multiple_of((1 - core) * tokens, tokens), tokens)] = other_ref[to]


def turn(kept, other):
    vmem = pl.BlockSpec(memory_space=pltpu.VMEM)
    chips, tokens, width = kept.shape
    return pl.pallas_call(
        turn_kernel,
        out_shape=(jax.ShapeDtypeStruct((2 * tokens, width), kept.dtype),) * chips,
        in_specs=[vmem, vmem],
        out_specs=(vmem,) * chips,
        compiler_params=pltpu.CompilerParams(vmem_limit_bytes=4 * 2**20),
        name="turn",
    )(kept, other)


def pack_kernel(own_ref, back_ref, out_ref):
    place = ROW * lax.axis_index("odd") + lax.axis_index("x")
    heads = out_ref.shape[1]
    for to in range(REACH):
        for head in range(heads):
            columns = slice(head * HEAD_WIDTH, (head + 1) * HEAD_WIDTH)
            out_ref[to, head] = jnp.where(to >= place, own_ref[:, columns], back_ref[:, columns])


def pack(own, back, heads):
    vmem = pl.BlockSpec(memory_space=pltpu.VMEM)
    return pl.pallas_call(
        pack_kernel,
        out_shape=jax.ShapeDtypeStruct((REACH, heads, own.shape[0], HEAD_WIDTH), own.dtype),
        in_specs=[vmem, vmem],
        out_specs=vmem,
        compiler_params=pltpu.CompilerParams(vmem_limit_bytes=4 * 2**20),
        name="pack",
    )(own, back)


def attend_kernel(begin_ref, *refs):
    parts, (pair_ref, out_ref, query_ref, score_a, score_b, hidden_ref) = refs[:-6], refs[-6:]
    y = lax.axis_index("y")
    for distance, part_ref in enumerate(parts):
        start = (y - distance + len(parts)) % len(parts) * part_ref.shape[0]
        query_ref[pl.ds(pl.multiple_of(start, part_ref.shape[0]), part_ref.shape[0])] = part_ref[...]
    place = ROW * lax.axis_index("odd") + lax.axis_index("x")
    block = REACH * lax.axis_index("z") + place
    rows = query_ref.shape[0]
    tile = (rows, rows)
    query_pos = block * rows + lax.broadcasted_iota(jnp.int32, tile, 0)
    lane = lax.broadcasted_iota(jnp.int32, tile, 1)
    begin = begin_ref[...]
    for j in range(REACH):
        first = block - place + jnp.where(j <= place, j, j - REACH)
        key_pos = first * rows + lane
        visible = (key_pos >= begin) & (key_pos <= query_pos)
        hidden_ref[:, j * rows : (j + 1) * rows] = jnp.where(visible, 0.0, HIDDEN)

    def scores(head, into):
        query = query_ref[:, head * HEAD_WIDTH : (head + 1) * HEAD_WIDTH]
        for j in range(REACH):
            key = pair_ref[j, :, 0].reshape(rows, HEAD_WIDTH)
            part = slice(j * rows, (j + 1) * rows)
            product = lax.dot_general(query, key, NT, preferred_element_type=jnp.float32)
            into[:, part] = product + hidden_ref[:, part]

    def output(head, score_ref):
        score = score_ref[...]
        top = jnp.max(score, axis=1, keepdims=True)
        probs = jnp.exp2((score - top) * EXP2_SCALE)
        total = jnp.sum(probs, axis=1, keepdims=True)
        probs = probs.astype(jnp.bfloat16)
        accum = jnp.zeros((rows, HEAD_WIDTH), jnp.float32)
        for j in range(REACH):
            value = pair_ref[j, :, 1].reshape(rows, HEAD_WIDTH)
            accum += jnp.dot(probs[:, j * rows : (j + 1) * rows], value, preferred_element_type=jnp.float32)
        out_ref[:, head * HEAD_WIDTH : (head + 1) * HEAD_WIDTH] = (accum / total).astype(jnp.bfloat16)

    buffers = (score_a, score_b)
    scores(0, score_a)
    for head in range(GROUP):
        if head + 1 < GROUP:
            scores(head + 1, buffers[(head + 1) % 2])
        output(head, buffers[head % 2])


def attend(begin, parts, pair):
    rows, width = begin.shape[0], parts[0].shape[1]
    vmem = pl.BlockSpec(memory_space=pltpu.VMEM)
    return pl.pallas_call(
        attend_kernel,
        out_shape=jax.ShapeDtypeStruct((rows, width), jnp.bfloat16),
        in_specs=[vmem] * (2 + len(parts)),
        out_specs=vmem,
        scratch_shapes=[pltpu.VMEM((rows, width), jnp.bfloat16)]
        + [pltpu.VMEM((rows, REACH * rows), jnp.float32)] * 3,
        compiler_params=pltpu.CompilerParams(vmem_limit_bytes=40 * 2**20),
        name="attend",
    )(begin, *parts, pair)


def body(queries, keys, values, doc_starts):
    tokens = queries.shape[0]
    n_y = lax.axis_size("y")
    n_tp = 2 * n_y
    rows = tokens * n_tp
    place = ROW * lax.axis_index("odd") + lax.axis_index("x")
    block = REACH * lax.axis_index("z") + place

    pair = join(keys, values)
    back = lax.ppermute(pair, "z", [(i, i + 1) for i in range(lax.axis_size("z") - 1)])
    sent = pack(pair, back, n_tp).reshape(REACH * n_tp, 2 * tokens, HEAD_WIDTH)
    got = lax.all_to_all(sent, ("odd", "x", "y", "core"), split_axis=0, concat_axis=0, tiled=True)
    got = got.reshape(REACH, n_tp, 2, tokens, HEAD_WIDTH)
    kept, given = halve(queries, n_y)
    other = lax.ppermute(given, "core", [(0, 1), (1, 0)])
    parts = list(turn(kept, other))
    for distance in range(1, n_y):
        route = [(i, (i + distance) % n_y) for i in range(n_y)]
        parts[distance] = lax.ppermute(parts[distance], "y", route)

    query_pos = block * rows + jnp.arange(rows, dtype=jnp.int32)
    begin = doc_begin(query_pos, doc_starts)[:, None]
    result = attend(begin, parts, got).reshape(n_tp, tokens, -1)
    return lax.all_to_all(result, ("y", "core"), split_axis=0, concat_axis=2, tiled=True)[0]


def solution(mesh):
    names = ("z", "odd", "x", "y", "core")
    split = Mesh(mesh.devices.reshape(-1, REACH // ROW, ROW, mesh.devices.shape[1] // 2, 2), names)
    whole = P(names, None)
    return jax.shard_map(body, mesh=split, in_specs=(whole, whole, whole, P()), out_specs=whole, check_vma=False)
```

time: 121 us -> 66.2 us (0.55)
  the two profiles are of different devices: /device:TPU:352 before, /device:TPU:1 now
where the time goes in v1:
time: 66.2 us; the launch traced here: 65.7 us
  starting transfers between devices  33 us (50%)
  blocking collectives  12.5 us (19%)
  waiting for transfers between devices  9.7 us (15%)
  Pallas kernels  9.28 us (14%)
  local copies, waits for them, and re-layouts  0.98 us (1%)
    all_to_all x1, starting transfers between devices, body(): lax.all_to_all(sent, ('odd', 'x', 'y', 'core'), split_axis=0, concat_axis...  14.3 us
    all_to_all x1, blocking collectives, body(): lax.all_to_all(result, ('y', 'core'), split_axis=0, concat_axis=2, tiled=...  12.5 us
    ppermute x3, starting transfers between devices, body(): parts[distance] = lax.ppermute(parts[distance], 'y', route)  10.5 us
    ppermute x3, waiting for transfers between devices, body(): parts[distance] = lax.ppermute(parts[distance], 'y', route)  6.64 us
    pallas_call x1, Pallas kernels, attend(): pl.pallas_call(attend_kernel, out_shape=jax.ShapeDtypeStruct((rows, width...  6 us
    ppermute x1, starting transfers between devices, body(): lax.ppermute(pair, 'z', [(i, i + 1) for i in range(lax.axis_size('z') - 1)])  5.72 us
    ppermute x1, starting transfers between devices, body(): other = lax.ppermute(given, 'core', [(0, 1), (1, 0)])  2.48 us
    ppermute x1, waiting for transfers between devices, body(): lax.ppermute(pair, 'z', [(i, i + 1) for i in range(lax.axis_size('z') - 1)])  1.92 us
  transfers between devices with their start and end apart: 6, of which 4 were waited for; matrix products, arithmetic and copies ran while one was open for 0% of the time, Pallas kernels for 2%

profile of v1, /device:TPU:1, one launch (start us, length us, event | category | flops | bytes accessed | tf_op | source)
XLA Modules:
  0.0 65.7 jit_solution(961046531021737440)
XLA Ops:
  0.0 0.9 %join.1.own_ref = bf16[64,1024]{1,0:T(8,128)(2,1)S(1)} custom-call(bf16[32,1024]{1,0:T(8,128)(2,1)} %key_ref.1, bf16[32,1024]{1,0:T(8,128)(2,1)} %value_ref.1), custom_call_target="tpu_custom_call" | custom-call | tf_op jit(solution)/shard_map/join/pallas_call | solution.py:43
  0.9 5.7 %collective-permute-start.4 = (bf16[64,1024]{1,0:T(8,128)(2,1)S(1)}, bf16[64,1024]{1,0:T(8,128)(2,1)S(1)}, u32[]{:S(2)}, u32[]{:S(2)}) collective-permute-start(bf16[64,1024]{1,0:T(8,128)(2,1)S(1)} %join.1.own_ref), channel_id=1, source_target_pairs={{0,64},{64,128},{128,192},{192,256},{256,320},{320,384},{384,448},... | collective-permute-start | bytes 393224 | tf_op jit(solution)/shard_map/ppermute | solution.py:197
  6.6 1.9 %collective-permute-done.4.back_ref = bf16[64,1024]{1,0:T(8,128)(2,1)S(1)} collective-permute-done((bf16[64,1024]{1,0:T(8,128)(2,1)S(1)}, bf16[64,1024]{1,0:T(8,128)(2,1)S(1)}, u32[]{:S(2)}, u32[]{:S(2)}) %collective-permute-start.4) | collective-permute-done | bytes 131104 | tf_op jit(solution)/shard_map/ppermute | solution.py:197
  8.5 1.2 %pack.1 = bf16[8,8,64,128]{3,2,1,0:T(8,128)(2,1)} custom-call(bf16[64,1024]{1,0:T(8,128)(2,1)S(1)} %join.1.own_ref, bf16[64,1024]{1,0:T(8,128)(2,1)S(1)} %collective-permute-done.4.back_ref), custom_call_target="tpu_custom_call" | custom-call | tf_op jit(solution)/shard_map/pack/pallas_call | solution.py:116
  9.8 14.3 %all-to-all-start = ((bf16[64,64,128]{2,1,0:T(8,128)(2,1)}), bf16[64,64,128]{2,1,0:T(8,128)(2,1)S(1)}, u32[]{:S(2)}, u32[]{:S(2)}) async-start(bf16[64,64,128]{2,1,0:T(8,128)(2,1)} %bitcast.1), calls=%async_computation | async-start | bytes 2097152 | tf_op jit(solution)/shard_map/all_to_all | solution.py:199
  24.1 1.1 %halve.1 = (bf16[4,32,1024]{2,1,0:T(8,128)(2,1)S(1)}, bf16[4,32,1024]{2,1,0:T(8,128)(2,1)S(1)}) custom-call(bf16[32,8192]{1,0:T(8,128)(2,1)} %query_ref.1), custom_call_target="tpu_custom_call" | custom-call | tf_op jit(solution)/shard_map/halve/pallas_call | solution.py:72
  25.3 2.5 %collective-permute-start = (bf16[4,32,1024]{2,1,0:T(8,128)(2,1)S(1)}, bf16[4,32,1024]{2,1,0:T(8,128)(2,1)S(1)}, u32[]{:S(2)}, u32[]{:S(2)}) collective-permute-start(bf16[4,32,1024]{2,1,0:T(8,128)(2,1)S(1)} %get-tuple-element.12), channel_id=1, source_target_pairs={{0,1},{1,0},{2,3},{3,2},{4,5},{5,4},{6,7},{7,6},{8,9},{9,8},{10,11... | collective-permute-start | bytes 786440 | tf_op jit(solution)/shard_map/ppermute | solution.py:202
  27.8 1.1 %collective-permute-done.other_ref = bf16[4,32,1024]{2,1,0:T(8,128)(2,1)S(1)} collective-permute-done((bf16[4,32,1024]{2,1,0:T(8,128)(2,1)S(1)}, bf16[4,32,1024]{2,1,0:T(8,128)(2,1)S(1)}, u32[]{:S(2)}, u32[]{:S(2)}) %collective-permute-start) | collective-permute-done | bytes 262176 | tf_op jit(solution)/shard_map/ppermute | solution.py:202
  28.9 3.1 %collective-permute-start.1 = (bf16[64,1024]{1,0:T(8,128)(2,1)S(1)}, bf16[64,1024]{1,0:T(8,128)(2,1)S(1)}, u32[]{:S(2)}, u32[]{:S(2)}) collective-permute-start(bf16[64,1024]{1,0:T(8,128)(2,1)S(1)} %get-tuple-element.14), channel_id=1, source_target_pairs={{0,2},{2,4},{4,6},{6,0},{1,3},{3,5},{5,7},{7,1},{8,10},{10,12},{12... | collective-permute-start | bytes 393224 | tf_op jit(solution)/shard_map/ppermute | solution.py:206
  32.0 4.3 %collective-permute-start.2 = (bf16[64,1024]{1,0:T(8,128)(2,1)S(1)}, bf16[64,1024]{1,0:T(8,128)(2,1)S(1)}, u32[]{:S(2)}, u32[]{:S(2)}) collective-permute-start(bf16[64,1024]{1,0:T(8,128)(2,1)S(1)} %get-tuple-element.15), channel_id=1, source_target_pairs={{0,4},{2,6},{4,0},{6,2},{1,5},{3,7},{5,1},{7,3},{8,12},{10,14},{12... | collective-permute-start | bytes 393224 | tf_op jit(solution)/shard_map/ppermute | solution.py:206
  36.4 0.0 copy-start
  36.4 3.1 %collective-permute-start.3 = (bf16[64,1024]{1,0:T(8,128)(2,1)S(1)}, bf16[64,1024]{1,0:T(8,128)(2,1)S(1)}, u32[]{:S(2)}, u32[]{:S(2)}) collective-permute-start(bf16[64,1024]{1,0:T(8,128)(2,1)S(1)} %get-tuple-element.16), channel_id=1, source_target_pairs={{0,6},{2,0},{4,2},{6,4},{1,7},{3,1},{5,3},{7,5},{8,14},{10,8},{12,... | collective-permute-start | bytes 393224 | tf_op jit(solution)/shard_map/ppermute | solution.py:206
  39.5 0.0 copy-done
  39.5 0.1 select_reduce_fusion
  39.6 0.1 copy.8.begin_ref
  39.7 3.3 %collective-permute-done.1.refs_1_ = bf16[64,1024]{1,0:T(8,128)(2,1)S(1)} collective-permute-done((bf16[64,1024]{1,0:T(8,128)(2,1)S(1)}, bf16[64,1024]{1,0:T(8,128)(2,1)S(1)}, u32[]{:S(2)}, u32[]{:S(2)}) %collective-permute-start.1) | collective-permute-done | bytes 131104 | tf_op jit(solution)/shard_map/ppermute | solution.py:206
  43.0 3.4 %collective-permute-done.2.refs_2_ = bf16[64,1024]{1,0:T(8,128)(2,1)S(1)} collective-permute-done((bf16[64,1024]{1,0:T(8,128)(2,1)S(1)}, bf16[64,1024]{1,0:T(8,128)(2,1)S(1)}, u32[]{:S(2)}, u32[]{:S(2)}) %collective-permute-start.2) | collective-permute-done | bytes 131104 | tf_op jit(solution)/shard_map/ppermute | solution.py:206
  46.4 0.0 collective-permute-done.3.refs_3_
  46.4 0.0 all-to-all-done
  46.4 6.0 %attend.1 = bf16[256,1024]{1,0:T(8,128)(2,1)S(1)} custom-call(s32[256,1]{1,0:T(8,128)S(1)} %copy.8.begin_ref, bf16[64,1024]{1,0:T(8,128)(2,1)S(1)} %get-tuple-element.13.refs_0_, bf16[64,1024]{1,0:T(8,128)(2,1)S(1)} %collective-permute-done.1.refs_1_, bf16[64,1024]{1,0:T(8,128)(2,1)S(1)} %collective-permute-done.2.refs_2_, ...), custom_call_target="tpu_custom_call" | custom-call | tf_op jit(solution)/shard_map/attend/pallas_call | solution.py:176
  52.4 12.5 %all_to_all.20 = bf16[8,32,1024]{2,1,0:T(8,128)(2,1)S(1)} all-to-all(bf16[8,32,1024]{2,1,0:T(8,128)(2,1)S(1)} %bitcast.13), channel_id=1, replica_groups=mesh['z'=16,'odd'=2,'x'=4,'y'=4,'core'=2] {'y','core'}, dimensions={0} | all-to-all | bytes 1048576 | tf_op jit(solution)/shard_map/all_to_all | solution.py:211
  64.9 0.8 %copy.10 = bf16[4,8,8,1024]{3,1,2,0:T(8,128)(2,1)} copy(bf16[4,8,8,1024]{3,1,0,2:T(8,128)(2,1)S(1)} %bitcast.14) | data formatting | bytes 1048576
  (2 shorter events, 0.0 us)
Async XLA Ops:
  0.9 7.7 %collective-permute-start.4 = (bf16[64,1024]{1,0:T(8,128)(2,1)S(1)}, bf16[64,1024]{1,0:T(8,128)(2,1)S(1)}, u32[]{:S(2)}, u32[]{:S(2)}) collective-permute-start(bf16[64,1024]{1,0:T(8,128)(2,1)S(1)} %join.1.own_ref), channel_id=1, source_target_pairs={{0,64},{64,128},{128,192},{192,256},{256,320},{320,384},{384,448},... | collective-permute-start | bytes 393224 | tf_op jit(solution)/shard_map/ppermute | solution.py:197
  9.8 36.6 %all-to-all-start = ((bf16[64,64,128]{2,1,0:T(8,128)(2,1)}), bf16[64,64,128]{2,1,0:T(8,128)(2,1)S(1)}, u32[]{:S(2)}, u32[]{:S(2)}) async-start(bf16[64,64,128]{2,1,0:T(8,128)(2,1)} %bitcast.1), calls=%async_computation | async-start | bytes 2097152 | tf_op jit(solution)/shard_map/all_to_all | solution.py:199
  25.3 3.6 %collective-permute-start = (bf16[4,32,1024]{2,1,0:T(8,128)(2,1)S(1)}, bf16[4,32,1024]{2,1,0:T(8,128)(2,1)S(1)}, u32[]{:S(2)}, u32[]{:S(2)}) collective-permute-start(bf16[4,32,1024]{2,1,0:T(8,128)(2,1)S(1)} %get-tuple-element.12), channel_id=1, source_target_pairs={{0,1},{1,0},{2,3},{3,2},{4,5},{5,4},{6,7},{7,6},{8,9},{9,8},{10,11... | collective-permute-start | bytes 786440 | tf_op jit(solution)/shard_map/ppermute | solution.py:202
  28.9 14.1 %collective-permute-start.1 = (bf16[64,1024]{1,0:T(8,128)(2,1)S(1)}, bf16[64,1024]{1,0:T(8,128)(2,1)S(1)}, u32[]{:S(2)}, u32[]{:S(2)}) collective-permute-start(bf16[64,1024]{1,0:T(8,128)(2,1)S(1)} %get-tuple-element.14), channel_id=1, source_target_pairs={{0,2},{2,4},{4,6},{6,0},{1,3},{3,5},{5,7},{7,1},{8,10},{10,12},{12... | collective-permute-start | bytes 393224 | tf_op jit(solution)/shard_map/ppermute | solution.py:206
  32.0 14.3 %collective-permute-start.2 = (bf16[64,1024]{1,0:T(8,128)(2,1)S(1)}, bf16[64,1024]{1,0:T(8,128)(2,1)S(1)}, u32[]{:S(2)}, u32[]{:S(2)}) collective-permute-start(bf16[64,1024]{1,0:T(8,128)(2,1)S(1)} %get-tuple-element.15), channel_id=1, source_target_pairs={{0,4},{2,6},{4,0},{6,2},{1,5},{3,7},{5,1},{7,3},{8,12},{10,14},{12... | collective-permute-start | bytes 393224 | tf_op jit(solution)/shard_map/ppermute | solution.py:206
  36.4 3.1 %copy-start = (s32[77]{0:T(128)S(1)}, s32[77]{0:T(128)}, u32[]{:S(2)}) copy-start(s32[77]{0:T(128)} %param.7) | copy-start | bytes 928
  36.4 10.0 %collective-permute-start.3 = (bf16[64,1024]{1,0:T(8,128)(2,1)S(1)}, bf16[64,1024]{1,0:T(8,128)(2,1)S(1)}, u32[]{:S(2)}, u32[]{:S(2)}) collective-permute-start(bf16[64,1024]{1,0:T(8,128)(2,1)S(1)} %get-tuple-element.16), channel_id=1, source_target_pairs={{0,6},{2,0},{4,2},{6,4},{1,7},{3,1},{5,3},{7,5},{8,14},{10,8},{12,... | collective-permute-start | bytes 393224 | tf_op jit(solution)/shard_map/ppermute | solution.py:206

commit v2 on v1

--- a/solution.py
+++ b/solution.py
@@ -1,3 +1,5 @@
+import functools
+
 import jax
 import jax.numpy as jnp
 from jax import lax
@@ -13,6 +15,8 @@
 ROW = 4
 REACH = 8
 HIDDEN = -1e30
+REACHES = (4, 6, 8)
+EARLY, LATE = (0, 2), (1, 3)
 EXP2_SCALE = HEAD_WIDTH ** (-0.5) * 1.4426950408889634
 NT = (((1,), (1,)), ((), ()))
 
@@ -123,66 +127,93 @@
     )(own, back)
 
 
-def attend_kernel(begin_ref, *refs):
-    parts, (pair_ref, out_ref, query_ref, score_a, score_b, hidden_ref) = refs[:-6], refs[-6:]
+def attend_kernel(distances, need_ref, begin_ref, *refs):
+    count = len(distances)
+    parts, (pair_ref, *done_refs, out_ref, query_ref, score_a, score_b, hidden_ref) = refs[:count], refs[count:]
     y = lax.axis_index("y")
-    for distance, part_ref in enumerate(parts):
-        start = (y - distance + len(parts)) % len(parts) * part_ref.shape[0]
-        query_ref[pl.ds(pl.multiple_of(start, part_ref.shape[0]), part_ref.shape[0])] = part_ref[...]
+    chips = lax.axis_size("y")
+    chunk = parts[0].shape[0]
+    rows, keys = query_ref.shape[0], score_a.shape[1] // REACH
+
+    def offset(distance):
+        return pl.multiple_of((y - distance + chips) % chips * chunk, chunk)
+
     place = ROW * lax.axis_index("odd") + lax.axis_index("x")
     block = REACH * lax.axis_index("z") + place
-    rows = query_ref.shape[0]
-    tile = (rows, rows)
-    query_pos = block * rows + lax.broadcasted_iota(jnp.int32, tile, 0)
-    lane = lax.broadcasted_iota(jnp.int32, tile, 1)
-    begin = begin_ref[...]
-    for j in range(REACH):
-        first = block - place + jnp.where(j <= place, j, j - REACH)
-        key_pos = first * rows + lane
-        visible = (key_pos >= begin) & (key_pos <= query_pos)
-        hidden_ref[:, j * rows : (j + 1) * rows] = jnp.where(visible, 0.0, HIDDEN)
-
-    def scores(head, into):
-        query = query_ref[:, head * HEAD_WIDTH : (head + 1) * HEAD_WIDTH]
-        for j in range(REACH):
-            key = pair_ref[j, :, 0].reshape(rows, HEAD_WIDTH)
-            part = slice(j * rows, (j + 1) * rows)
-            product = lax.dot_general(query, key, NT, preferred_element_type=jnp.float32)
-            into[:, part] = product + hidden_ref[:, part]
-
-    def output(head, score_ref):
-        score = score_ref[...]
-        top = jnp.max(score, axis=1, keepdims=True)
-        probs = jnp.exp2((score - top) * EXP2_SCALE)
-        total = jnp.sum(probs, axis=1, keepdims=True)
-        probs = probs.astype(jnp.bfloat16)
-        accum = jnp.zeros((rows, HEAD_WIDTH), jnp.float32)
-        for j in range(REACH):
-            value = pair_ref[j, :, 1].reshape(rows, HEAD_WIDTH)
-            accum += jnp.dot(probs[:, j * rows : (j + 1) * rows], value, preferred_element_type=jnp.float32)
-        out_ref[:, head * HEAD_WIDTH : (head + 1) * HEAD_WIDTH] = (accum / total).astype(jnp.bfloat16)
-
-    buffers = (score_a, score_b)
-    scores(0, score_a)
-    for head in range(GROUP):
-        if head + 1 < GROUP:
-            scores(head + 1, buffers[(head + 1) % 2])
-        output(head, buffers[head % 2])
-
-
-def attend(begin, parts, pair):
-    rows, width = begin.shape[0], parts[0].shape[1]
+    for i, part_ref in enumerate(parts):
+        query_ref[i * chunk : (i + 1) * chunk] = part_ref[...]
+    if done_refs:
+        for i, distance in enumerate(EARLY):
+            out_ref[pl.ds(offset(distance), chunk)] = done_refs[0][i * chunk : (i + 1) * chunk]
+
+    def over(reach):
+        if reach == REACH:
+            slots = list(range(REACH))
+            blocks = [block - place + jnp.where(j <= place, j, j - REACH) for j in slots]
+        else:
+            slots = [(place + REACH - reach + 1 + j) % REACH for j in range(reach)]
+            blocks = [block - reach + 1 + j for j in range(reach)]
+        lane = lax.broadcasted_iota(jnp.int32, (chunk, keys), 1)
+        for i, distance in enumerate(distances):
+            begin = begin_ref[pl.ds(offset(distance), chunk)]
+            query_pos = block * keys + offset(distance) + lax.broadcasted_iota(jnp.int32, (chunk, keys), 0)
+            for j in range(reach):
+                key_pos = blocks[j] * keys + lane
+                visible = (key_pos >= begin) & (key_pos <= query_pos)
+                hidden_ref[i * chunk : (i + 1) * chunk, j * keys : (j + 1) * keys] = jnp.where(visible, 0.0, HIDDEN)
+
+        def scores(head, into):
+            query = query_ref[:, head * HEAD_WIDTH : (head + 1) * HEAD_WIDTH]
+            for j in range(reach):
+                key = pair_ref[slots[j], :, 0].reshape(keys, HEAD_WIDTH)
+                part = slice(j * keys, (j + 1) * keys)
+                product = lax.dot_general(query, key, NT, preferred_element_type=jnp.float32)
+                into[:, part] = product + hidden_ref[:, part]
+
+        def output(head, score_ref):
+            score = score_ref[:, : reach * keys]
+            top = jnp.max(score, axis=1, keepdims=True)
+            probs = jnp.exp2((score - top) * EXP2_SCALE)
+            total = jnp.sum(probs, axis=1, keepdims=True)
+            probs = probs.astype(jnp.bfloat16)
+            accum = jnp.zeros((rows, HEAD_WIDTH), jnp.float32)
+            for j in range(reach):
+                value = pair_ref[slots[j], :, 1].reshape(keys, HEAD_WIDTH)
+                accum += jnp.dot(probs[:, j * keys : (j + 1) * keys], value, preferred_element_type=jnp.float32)
+            result = (accum / total).astype(jnp.bfloat16)
+            columns = slice(head * HEAD_WIDTH, (head + 1) * HEAD_WIDTH)
+            if out_ref.shape[0] == rows:
+                out_ref[:, columns] = result
+            else:
+                for i, distance in enumerate(distances):
+                    out_ref[pl.ds(offset(distance), chunk), columns] = result[i * chunk : (i + 1) * chunk]
+
+        buffers = (score_a, score_b)
+        scores(0, score_a)
+        for head in range(GROUP):
+            if head + 1 < GROUP:
+                scores(head + 1, buffers[(head + 1) % 2])
+            output(head, buffers[head % 2])
+
+    need = need_ref[0]
+    for less, reach in zip((0,) + REACHES, REACHES):
+        pl.when((need > less) & (need <= reach))(functools.partial(over, reach))
+
+
+def attend(distances, need, begin, parts, pair, *done):
+    keys, width = begin.shape[0], parts[0].shape[1]
+    rows = len(parts) * parts[0].shape[0]
     vmem = pl.BlockSpec(memory_space=pltpu.VMEM)
     return pl.pallas_call(
-        attend_kernel,
-        out_shape=jax.ShapeDtypeStruct((rows, width), jnp.bfloat16),
-        in_specs=[vmem] * (2 + len(parts)),
+        functools.partial(attend_kernel, distances),
+        out_shape=jax.ShapeDtypeStruct((keys if done else rows, width), jnp.bfloat16),
+        in_specs=[pl.BlockSpec(memory_space=pltpu.SMEM)] + [vmem] * (2 + len(parts) + len(done)),
         out_specs=vmem,
         scratch_shapes=[pltpu.VMEM((rows, width), jnp.bfloat16)]
-        + [pltpu.VMEM((rows, REACH * rows), jnp.float32)] * 3,
-        compiler_params=pltpu.CompilerParams(vmem_limit_bytes=40 * 2**20),
+        + [pltpu.VMEM((rows, REACH * keys), jnp.float32)] * 3,
+        compiler_params=pltpu.CompilerParams(vmem_limit_bytes=20 * 2**20),
         name="attend",
-    )(begin, *parts, pair)
+    )(need, begin, *parts, pair, *done)
 
 
 def body(queries, keys, values, doc_starts):
@@ -206,8 +237,12 @@
         parts[distance] = lax.ppermute(parts[distance], "y", route)
 
     query_pos = block * rows + jnp.arange(rows, dtype=jnp.int32)
-    begin = doc_begin(query_pos, doc_starts)[:, None]
-    result = attend(begin, parts, got).reshape(n_tp, tokens, -1)
+    begin = doc_begin(query_pos, doc_starts)
+    need = block + 1 - begin[:1] // rows
+    begin = begin[:, None]
+    early = attend(EARLY, need, begin, [parts[d] for d in EARLY], got)
+    result = attend(LATE, need, begin, [parts[d] for d in LATE], got, early)
+    result = result.reshape(n_tp, tokens, -1)
     return lax.all_to_all(result, ("y", "core"), split_axis=0, concat_axis=2, tiled=True)[0]
 
 

time: 66.2 us -> 64.6 us (0.976)
  the two profiles are of different devices: /device:TPU:1 before, /device:TPU:36 now
where the time goes in v2:
time: 64.6 us; the launch traced here: 64.1 us
  starting transfers between devices  28.5 us (44%)
  blocking collectives  12.8 us (20%)
  Pallas kernels  10.1 us (16%)
  waiting for transfers between devices  8.4 us (13%)
  between operations  2.65 us (4%)
  local copies, waits for them, and re-layouts  1.55 us (2%)
    all_to_all x1, blocking collectives, body(): lax.all_to_all(result, ('y', 'core'), split_axis=0, concat_axis=2, tiled=...  12.8 us
    ppermute x3, starting transfers between devices, body(): parts[distance] = lax.ppermute(parts[distance], 'y', route)  10.7 us
    all_to_all x1, starting transfers between devices, body(): lax.all_to_all(sent, ('odd', 'x', 'y', 'core'), split_axis=0, concat_axis...  10.6 us
    pallas_call x2, Pallas kernels, attend(): pl.pallas_call(functools.partial(attend_kernel, distances), out_shape=jax...  6.82 us
    ppermute x1, starting transfers between devices, body(): lax.ppermute(pair, 'z', [(i, i + 1) for i in range(lax.axis_size('z') - 1)])  5.18 us
    ppermute x1, waiting for transfers between devices, body(): lax.ppermute(pair, 'z', [(i, i + 1) for i in range(lax.axis_size('z') - 1)])  5.13 us
    ppermute x1, starting transfers between devices, body(): other = lax.ppermute(given, 'core', [(0, 1), (1, 0)])  2.03 us
    ppermute x3, waiting for transfers between devices, body(): parts[distance] = lax.ppermute(parts[distance], 'y', route)  1.88 us
  transfers between devices with their start and end apart: 6, of which 3 were waited for; matrix products, arithmetic and copies ran while one was open for 1% of the time, Pallas kernels for 7%

profile of v2, /device:TPU:36, one launch (start us, length us, event | category | flops | bytes accessed | tf_op | source)
XLA Modules:
  0.0 64.1 jit_solution(2211653079495730892)
XLA Ops:
  0.0 0.9 %join.1.own_ref = bf16[64,1024]{1,0:T(8,128)(2,1)S(1)} custom-call(bf16[32,1024]{1,0:T(8,128)(2,1)} %key_ref.1, bf16[32,1024]{1,0:T(8,128)(2,1)} %value_ref.1), custom_call_target="tpu_custom_call" | custom-call | tf_op jit(solution)/shard_map/join/pallas_call | solution.py:47
  0.9 5.2 %collective-permute-start.3 = (bf16[64,1024]{1,0:T(8,128)(2,1)S(1)}, bf16[64,1024]{1,0:T(8,128)(2,1)S(1)}, u32[]{:S(2)}, u32[]{:S(2)}) collective-permute-start(bf16[64,1024]{1,0:T(8,128)(2,1)S(1)} %join.1.own_ref), channel_id=1, source_target_pairs={{0,64},{64,128},{128,192},{192,256},{256,320},{320,384},{384,448},... | collective-permute-start | bytes 393224 | tf_op jit(solution)/shard_map/ppermute | solution.py:228
  6.1 5.1 %collective-permute-done.3.back_ref = bf16[64,1024]{1,0:T(8,128)(2,1)S(1)} collective-permute-done((bf16[64,1024]{1,0:T(8,128)(2,1)S(1)}, bf16[64,1024]{1,0:T(8,128)(2,1)S(1)}, u32[]{:S(2)}, u32[]{:S(2)}) %collective-permute-start.3) | collective-permute-done | bytes 131104 | tf_op jit(solution)/shard_map/ppermute | solution.py:228
  11.2 1.2 %pack.1 = bf16[8,8,64,128]{3,2,1,0:T(8,128)(2,1)} custom-call(bf16[64,1024]{1,0:T(8,128)(2,1)S(1)} %join.1.own_ref, bf16[64,1024]{1,0:T(8,128)(2,1)S(1)} %collective-permute-done.3.back_ref), custom_call_target="tpu_custom_call" | custom-call | tf_op jit(solution)/shard_map/pack/pallas_call | solution.py:120
  12.4 10.6 %all-to-all-start = ((bf16[64,64,128]{2,1,0:T(8,128)(2,1)}), bf16[64,64,128]{2,1,0:T(8,128)(2,1)S(1)}, u32[]{:S(2)}, u32[]{:S(2)}) async-start(bf16[64,64,128]{2,1,0:T(8,128)(2,1)} %bitcast.2), calls=%async_computation | async-start | bytes 2097152 | tf_op jit(solution)/shard_map/all_to_all | solution.py:230
  23.0 1.1 %halve.1 = (bf16[4,32,1024]{2,1,0:T(8,128)(2,1)S(1)}, bf16[4,32,1024]{2,1,0:T(8,128)(2,1)S(1)}) custom-call(bf16[32,8192]{1,0:T(8,128)(2,1)} %query_ref.1), custom_call_target="tpu_custom_call" | custom-call | tf_op jit(solution)/shard_map/halve/pallas_call | solution.py:76
  24.2 2.0 %collective-permute-start = (bf16[4,32,1024]{2,1,0:T(8,128)(2,1)S(1)}, bf16[4,32,1024]{2,1,0:T(8,128)(2,1)S(1)}, u32[]{:S(2)}, u32[]{:S(2)}) collective-permute-start(bf16[4,32,1024]{2,1,0:T(8,128)(2,1)S(1)} %get-tuple-element.12), channel_id=1, source_target_pairs={{0,1},{1,0},{2,3},{3,2},{4,5},{5,4},{6,7},{7,6},{8,9},{9,8},{10,11... | collective-permute-start | bytes 786440 | tf_op jit(solution)/shard_map/ppermute | solution.py:233
  26.2 1.4 %collective-permute-done.other_ref = bf16[4,32,1024]{2,1,0:T(8,128)(2,1)S(1)} collective-permute-done((bf16[4,32,1024]{2,1,0:T(8,128)(2,1)S(1)}, bf16[4,32,1024]{2,1,0:T(8,128)(2,1)S(1)}, u32[]{:S(2)}, u32[]{:S(2)}) %collective-permute-start) | collective-permute-done | bytes 262176 | tf_op jit(solution)/shard_map/ppermute | solution.py:233
  27.6 3.4 %collective-permute-start.1 = (bf16[64,1024]{1,0:T(8,128)(2,1)S(1)}, bf16[64,1024]{1,0:T(8,128)(2,1)S(1)}, u32[]{:S(2)}, u32[]{:S(2)}) collective-permute-start(bf16[64,1024]{1,0:T(8,128)(2,1)S(1)} %get-tuple-element.13), channel_id=1, source_target_pairs={{0,2},{2,4},{4,6},{6,0},{1,3},{3,5},{5,7},{7,1},{8,10},{10,12},{12... | collective-permute-start | bytes 393224 | tf_op jit(solution)/shard_map/ppermute | solution.py:237
  31.0 3.7 %collective-permute-start.2 = (bf16[64,1024]{1,0:T(8,128)(2,1)S(1)}, bf16[64,1024]{1,0:T(8,128)(2,1)S(1)}, u32[]{:S(2)}, u32[]{:S(2)}) collective-permute-start(bf16[64,1024]{1,0:T(8,128)(2,1)S(1)} %get-tuple-element.14), channel_id=1, source_target_pairs={{0,6},{2,0},{4,2},{6,4},{1,7},{3,1},{5,3},{7,5},{8,14},{10,8},{12,... | collective-permute-start | bytes 393224 | tf_op jit(solution)/shard_map/ppermute | solution.py:237
  34.7 0.0 copy-start
  34.7 3.7 %collective-permute-start.4 = (bf16[64,1024]{1,0:T(8,128)(2,1)S(1)}, bf16[64,1024]{1,0:T(8,128)(2,1)S(1)}, u32[]{:S(2)}, u32[]{:S(2)}) collective-permute-start(bf16[64,1024]{1,0:T(8,128)(2,1)S(1)} %get-tuple-element.16), channel_id=1, source_target_pairs={{0,4},{2,6},{4,0},{6,2},{1,5},{3,7},{5,1},{7,3},{8,12},{10,14},{12... | collective-permute-start | bytes 393224 | tf_op jit(solution)/shard_map/ppermute | solution.py:237
  38.4 0.0 copy-done
  38.4 0.1 select_reduce_fusion
  38.5 0.6 slice.3
  41.6 0.1 copy.10.begin_ref
  41.8 1.9 %collective-permute-done.4.refs_1_ = bf16[64,1024]{1,0:T(8,128)(2,1)S(1)} collective-permute-done((bf16[64,1024]{1,0:T(8,128)(2,1)S(1)}, bf16[64,1024]{1,0:T(8,128)(2,1)S(1)}, u32[]{:S(2)}, u32[]{:S(2)}) %collective-permute-start.4) | collective-permute-done | bytes 131104 | tf_op jit(solution)/shard_map/ppermute | solution.py:237
  43.6 0.0 all-to-all-done
  43.6 3.3 %attend.2.refs_3_ = bf16[128,1024]{1,0:T(8,128)(2,1)S(1)} custom-call(s32[1]{0:T(128)S(6)} %sub.12.need_ref, s32[256,1]{1,0:T(8,128)S(1)} %copy.10.begin_ref, bf16[64,1024]{1,0:T(8,128)(2,1)S(1)} %get-tuple-element.15.refs_0_, bf16[64,1024]{1,0:T(8,128)(2,1)S(1)} %collective-permute-done.4.refs_1_, bf16[8,8,2,32,128]{4,3,2,1,0:T(8,128)(2,1)S(1)} %bitcast.13), custom_call_target="tpu_custom_call" | custom-call | tf_op jit(solution)/shard_map/attend/pallas_call | solution.py:207
  46.9 0.0 collective-permute-done.1.refs_0_
  47.0 0.0 collective-permute-done.2.refs_1_
  47.0 3.5 %attend.3 = bf16[256,1024]{1,0:T(8,128)(2,1)S(1)} custom-call(s32[1]{0:T(128)S(6)} %sub.12.need_ref, s32[256,1]{1,0:T(8,128)S(1)} %copy.10.begin_ref, bf16[64,1024]{1,0:T(8,128)(2,1)S(1)} %collective-permute-done.1.refs_0_, bf16[64,1024]{1,0:T(8,128)(2,1)S(1)} %collective-permute-done.2.refs_1_, bf16[8,8,2,32,128]{4,3,2,1,0:T(8,128)(2,1)S(1)} %bitcast.14, ...), custom_call_target="tpu_custom_call" | custom-call | tf_op jit(solution)/shard_map/attend/pallas_call | solution.py:207
  50.5 12.8 %all_to_all.20 = bf16[8,32,1024]{2,1,0:T(8,128)(2,1)S(1)} all-to-all(bf16[8,32,1024]{2,1,0:T(8,128)(2,1)S(1)} %bitcast.15), channel_id=1, replica_groups=mesh['z'=16,'odd'=2,'x'=4,'y'=4,'core'=2] {'y','core'}, dimensions={0} | all-to-all | bytes 1048576 | tf_op jit(solution)/shard_map/all_to_all | solution.py:246
  63.3 0.8 %copy.12 = bf16[4,8,8,1024]{3,1,2,0:T(8,128)(2,1)} copy(bf16[4,8,8,1024]{3,1,0,2:T(8,128)(2,1)S(1)} %bitcast.16) | data formatting | bytes 1048576
  (2 shorter events, 0.0 us)
Async XLA Ops:
  0.9 10.3 %collective-permute-start.3 = (bf16[64,1024]{1,0:T(8,128)(2,1)S(1)}, bf16[64,1024]{1,0:T(8,128)(2,1)S(1)}, u32[]{:S(2)}, u32[]{:S(2)}) collective-permute-start(bf16[64,1024]{1,0:T(8,128)(2,1)S(1)} %join.1.own_ref), channel_id=1, source_target_pairs={{0,64},{64,128},{128,192},{192,256},{256,320},{320,384},{384,448},... | collective-permute-start | bytes 393224 | tf_op jit(solution)/shard_map/ppermute | solution.py:228
  12.4 31.2 %all-to-all-start = ((bf16[64,64,128]{2,1,0:T(8,128)(2,1)}), bf16[64,64,128]{2,1,0:T(8,128)(2,1)S(1)}, u32[]{:S(2)}, u32[]{:S(2)}) async-start(bf16[64,64,128]{2,1,0:T(8,128)(2,1)} %bitcast.2), calls=%async_computation | async-start | bytes 2097152 | tf_op jit(solution)/shard_map/all_to_all | solution.py:230
  24.2 3.4 %collective-permute-start = (bf16[4,32,1024]{2,1,0:T(8,128)(2,1)S(1)}, bf16[4,32,1024]{2,1,0:T(8,128)(2,1)S(1)}, u32[]{:S(2)}, u32[]{:S(2)}) collective-permute-start(bf16[4,32,1024]{2,1,0:T(8,128)(2,1)S(1)} %get-tuple-element.12), channel_id=1, source_target_pairs={{0,1},{1,0},{2,3},{3,2},{4,5},{5,4},{6,7},{7,6},{8,9},{9,8},{10,11... | collective-permute-start | bytes 786440 | tf_op jit(solution)/shard_map/ppermute | solution.py:233
  27.6 19.3 %collective-permute-start.1 = (bf16[64,1024]{1,0:T(8,128)(2,1)S(1)}, bf16[64,1024]{1,0:T(8,128)(2,1)S(1)}, u32[]{:S(2)}, u32[]{:S(2)}) collective-permute-start(bf16[64,1024]{1,0:T(8,128)(2,1)S(1)} %get-tuple-element.13), channel_id=1, source_target_pairs={{0,2},{2,4},{4,6},{6,0},{1,3},{3,5},{5,7},{7,1},{8,10},{10,12},{12... | collective-permute-start | bytes 393224 | tf_op jit(solution)/shard_map/ppermute | solution.py:237
  31.0 15.9 %collective-permute-start.2 = (bf16[64,1024]{1,0:T(8,128)(2,1)S(1)}, bf16[64,1024]{1,0:T(8,128)(2,1)S(1)}, u32[]{:S(2)}, u32[]{:S(2)}) collective-permute-start(bf16[64,1024]{1,0:T(8,128)(2,1)S(1)} %get-tuple-element.14), channel_id=1, source_target_pairs={{0,6},{2,0},{4,2},{6,4},{1,7},{3,1},{5,3},{7,5},{8,14},{10,8},{12,... | collective-permute-start | bytes 393224 | tf_op jit(solution)/shard_map/ppermute | solution.py:237
  34.7 3.7 %copy-start = (s32[77]{0:T(128)S(1)}, s32[77]{0:T(128)}, u32[]{:S(2)}) copy-start(s32[77]{0:T(128)} %param.7) | copy-start | bytes 928
  34.7 8.9 %collective-permute-start.4 = (bf16[64,1024]{1,0:T(8,128)(2,1)S(1)}, bf16[64,1024]{1,0:T(8,128)(2,1)S(1)}, u32[]{:S(2)}, u32[]{:S(2)}) collective-permute-start(bf16[64,1024]{1,0:T(8,128)(2,1)S(1)} %get-tuple-element.16), channel_id=1, source_target_pairs={{0,4},{2,6},{4,0},{6,2},{1,5},{3,7},{5,1},{7,3},{8,12},{10,14},{12... | collective-permute-start | bytes 393224 | tf_op jit(solution)/shard_map/ppermute | solution.py:237

commit v3 on v2

--- a/solution.py
+++ b/solution.py
@@ -15,6 +15,7 @@
 ROW = 4
 REACH = 8
 HIDDEN = -1e30
+ORDER = ("y", "core", "odd", "x")
 REACHES = (4, 6, 8)
 EARLY, LATE = (0, 2), (1, 3)
 EXP2_SCALE = HEAD_WIDTH ** (-0.5) * 1.4426950408889634
@@ -106,20 +107,29 @@
     )(kept, other)
 
 
+def peer(place, head):
+    sizes = {"odd": REACH // ROW, "x": ROW, "y": KEY_VALUE_HEADS // 2, "core": 2}
+    at = {"odd": place // ROW, "x": place % ROW, "y": head // 2, "core": head % 2}
+    index = 0
+    for axis in ORDER:
+        index = index * sizes[axis] + at[axis]
+    return index
+
+
 def pack_kernel(own_ref, back_ref, out_ref):
     place = ROW * lax.axis_index("odd") + lax.axis_index("x")
-    heads = out_ref.shape[1]
+    heads = out_ref.shape[0] // REACH
     for to in range(REACH):
         for head in range(heads):
             columns = slice(head * HEAD_WIDTH, (head + 1) * HEAD_WIDTH)
-            out_ref[to, head] = jnp.where(to >= place, own_ref[:, columns], back_ref[:, columns])
+            out_ref[peer(to, head)] = jnp.where(to >= place, own_ref[:, columns], back_ref[:, columns])
 
 
 def pack(own, back, heads):
     vmem = pl.BlockSpec(memory_space=pltpu.VMEM)
     return pl.pallas_call(
         pack_kernel,
-        out_shape=jax.ShapeDtypeStruct((REACH, heads, own.shape[0], HEAD_WIDTH), own.dtype),
+        out_shape=jax.ShapeDtypeStruct((REACH * heads, own.shape[0], HEAD_WIDTH), own.dtype),
         in_specs=[vmem, vmem],
         out_specs=vmem,
         compiler_params=pltpu.CompilerParams(vmem_limit_bytes=4 * 2**20),
@@ -145,6 +155,10 @@
     if done_refs:
         for i, distance in enumerate(EARLY):
             out_ref[pl.ds(offset(distance), chunk)] = done_refs[0][i * chunk : (i + 1) * chunk]
+
+    def gathered(slot, which):
+        pieces = [pair_ref[peer(slot, piece), which] for piece in range(KEY_VALUE_HEADS)]
+        return jnp.concatenate(pieces, axis=0)
 
     def over(reach):
         if reach == REACH:
@@ -165,7 +179,7 @@
         def scores(head, into):
             query = query_ref[:, head * HEAD_WIDTH : (head + 1) * HEAD_WIDTH]
             for j in range(reach):
-                key = pair_ref[slots[j], :, 0].reshape(keys, HEAD_WIDTH)
+                key = gathered(slots[j], 0)
                 part = slice(j * keys, (j + 1) * keys)
                 product = lax.dot_general(query, key, NT, preferred_element_type=jnp.float32)
                 into[:, part] = product + hidden_ref[:, part]
@@ -178,7 +192,7 @@
             probs = probs.astype(jnp.bfloat16)
             accum = jnp.zeros((rows, HEAD_WIDTH), jnp.float32)
             for j in range(reach):
-                value = pair_ref[slots[j], :, 1].reshape(keys, HEAD_WIDTH)
+                value = gathered(slots[j], 1)
                 accum += jnp.dot(probs[:, j * keys : (j + 1) * keys], value, preferred_element_type=jnp.float32)
             result = (accum / total).astype(jnp.bfloat16)
             columns = slice(head * HEAD_WIDTH, (head + 1) * HEAD_WIDTH)
@@ -226,9 +240,9 @@
 
     pair = join(keys, values)
     back = lax.ppermute(pair, "z", [(i, i + 1) for i in range(lax.axis_size("z") - 1)])
-    sent = pack(pair, back, n_tp).reshape(REACH * n_tp, 2 * tokens, HEAD_WIDTH)
-    got = lax.all_to_all(sent, ("odd", "x", "y", "core"), split_axis=0, concat_axis=0, tiled=True)
-    got = got.reshape(REACH, n_tp, 2, tokens, HEAD_WIDTH)
+    sent = pack(pair, back, n_tp)
+    got = lax.all_to_all(sent, ORDER, split_axis=0, concat_axis=0, tiled=True)
+    got = got.reshape(REACH * n_tp, 2, tokens, HEAD_WIDTH)
     kept, given = halve(queries, n_y)
     other = lax.ppermute(given, "core", [(0, 1), (1, 0)])
     parts = list(turn(kept, other))
@@ -238,7 +252,7 @@
 
     query_pos = block * rows + jnp.arange(rows, dtype=jnp.int32)
     begin = doc_begin(query_pos, doc_starts)
-    need = block + 1 - begin[:1] // rows
+    need = jnp.minimum(block + 1 - begin[:1] // rows, REACH)
     begin = begin[:, None]
     early = attend(EARLY, need, begin, [parts[d] for d in EARLY], got)
     result = attend(LATE, need, begin, [parts[d] for d in LATE], got, early)

time: 64.6 us -> 64.6 us (level)
  the two profiles are of different devices: /device:TPU:36 before, /device:TPU:96 now
where the time goes in v3:
time: 64.6 us; the launch traced here: 64.1 us
  starting transfers between devices  28.2 us (44%)
  blocking collectives  12.8 us (20%)
  waiting for transfers between devices  10.4 us (16%)
  Pallas kernels  8.45 us (13%)
  between operations  2.64 us (4%)
  local copies, waits for them, and re-layouts  1.55 us (2%)
    all_to_all x1, blocking collectives, body(): lax.all_to_all(result, ('y', 'core'), split_axis=0, concat_axis=2, tiled=...  12.8 us
    ppermute x3, starting transfers between devices, body(): parts[distance] = lax.ppermute(parts[distance], 'y', route)  10.9 us
    all_to_all x1, starting transfers between devices, body(): got = lax.all_to_all(sent, ORDER, split_axis=0, concat_axis=0, tiled=True)  8.78 us
    ppermute x1, starting transfers between devices, body(): lax.ppermute(pair, 'z', [(i, i + 1) for i in range(lax.axis_size('z') - 1)])  6.39 us
    ppermute x1, waiting for transfers between devices, body(): lax.ppermute(pair, 'z', [(i, i + 1) for i in range(lax.axis_size('z') - 1)])  5.53 us
    pallas_call x2, Pallas kernels, attend(): pl.pallas_call(functools.partial(attend_kernel, distances), out_shape=jax...  5.17 us
    ppermute x3, waiting for transfers between devices, body(): parts[distance] = lax.ppermute(parts[distance], 'y', route)  3.57 us
    ppermute x1, starting transfers between devices, body(): other = lax.ppermute(given, 'core', [(0, 1), (1, 0)])  2.08 us
  transfers between devices with their start and end apart: 6, of which 3 were waited for; matrix products, arithmetic and copies ran while one was open for 1% of the time, Pallas kernels for 6%

profile of v3, /device:TPU:96, one launch (start us, length us, event | category | flops | bytes accessed | tf_op | source)
XLA Modules:
  0.0 64.1 jit_solution(2246848440557303773)
XLA Ops:
  0.0 0.9 %join.1.own_ref = bf16[64,1024]{1,0:T(8,128)(2,1)S(1)} custom-call(bf16[32,1024]{1,0:T(8,128)(2,1)} %key_ref.1, bf16[32,1024]{1,0:T(8,128)(2,1)} %value_ref.1), custom_call_target="tpu_custom_call" | custom-call | tf_op jit(solution)/shard_map/join/pallas_call | solution.py:48
  0.9 6.4 %collective-permute-start.3 = (bf16[64,1024]{1,0:T(8,128)(2,1)S(1)}, bf16[64,1024]{1,0:T(8,128)(2,1)S(1)}, u32[]{:S(2)}, u32[]{:S(2)}) collective-permute-start(bf16[64,1024]{1,0:T(8,128)(2,1)S(1)} %join.1.own_ref), channel_id=1, source_target_pairs={{0,64},{64,128},{128,192},{192,256},{256,320},{320,384},{384,448},... | collective-permute-start | bytes 393224 | tf_op jit(solution)/shard_map/ppermute | solution.py:242
  7.3 5.5 %collective-permute-done.3.back_ref = bf16[64,1024]{1,0:T(8,128)(2,1)S(1)} collective-permute-done((bf16[64,1024]{1,0:T(8,128)(2,1)S(1)}, bf16[64,1024]{1,0:T(8,128)(2,1)S(1)}, u32[]{:S(2)}, u32[]{:S(2)}) %collective-permute-start.3) | collective-permute-done | bytes 131104 | tf_op jit(solution)/shard_map/ppermute | solution.py:242
  12.8 1.2 %pack.1 = bf16[64,64,128]{2,1,0:T(8,128)(2,1)} custom-call(bf16[64,1024]{1,0:T(8,128)(2,1)S(1)} %join.1.own_ref, bf16[64,1024]{1,0:T(8,128)(2,1)S(1)} %collective-permute-done.3.back_ref), custom_call_target="tpu_custom_call" | custom-call | tf_op jit(solution)/shard_map/pack/pallas_call | solution.py:130
  14.0 8.8 %all-to-all-start = ((bf16[64,64,128]{2,1,0:T(8,128)(2,1)}), bf16[64,64,128]{2,1,0:T(8,128)(2,1)S(1)}, u32[]{:S(2)}, u32[]{:S(2)}) async-start(bf16[64,64,128]{2,1,0:T(8,128)(2,1)} %pack.1), calls=%async_computation | async-start | bytes 2097152 | tf_op jit(solution)/shard_map/all_to_all | solution.py:244
  22.8 1.1 %halve.1 = (bf16[4,32,1024]{2,1,0:T(8,128)(2,1)S(1)}, bf16[4,32,1024]{2,1,0:T(8,128)(2,1)S(1)}) custom-call(bf16[32,8192]{1,0:T(8,128)(2,1)} %query_ref.1), custom_call_target="tpu_custom_call" | custom-call | tf_op jit(solution)/shard_map/halve/pallas_call | solution.py:77
  24.0 2.1 %collective-permute-start = (bf16[4,32,1024]{2,1,0:T(8,128)(2,1)S(1)}, bf16[4,32,1024]{2,1,0:T(8,128)(2,1)S(1)}, u32[]{:S(2)}, u32[]{:S(2)}) collective-permute-start(bf16[4,32,1024]{2,1,0:T(8,128)(2,1)S(1)} %get-tuple-element.12), channel_id=1, source_target_pairs={{0,1},{1,0},{2,3},{3,2},{4,5},{5,4},{6,7},{7,6},{8,9},{9,8},{10,11... | collective-permute-start | bytes 786440 | tf_op jit(solution)/shard_map/ppermute | solution.py:247
  26.1 1.3 %collective-permute-done.other_ref = bf16[4,32,1024]{2,1,0:T(8,128)(2,1)S(1)} collective-permute-done((bf16[4,32,1024]{2,1,0:T(8,128)(2,1)S(1)}, bf16[4,32,1024]{2,1,0:T(8,128)(2,1)S(1)}, u32[]{:S(2)}, u32[]{:S(2)}) %collective-permute-start) | collective-permute-done | bytes 262176 | tf_op jit(solution)/shard_map/ppermute | solution.py:247
  27.5 3.5 %collective-permute-start.1 = (bf16[64,1024]{1,0:T(8,128)(2,1)S(1)}, bf16[64,1024]{1,0:T(8,128)(2,1)S(1)}, u32[]{:S(2)}, u32[]{:S(2)}) collective-permute-start(bf16[64,1024]{1,0:T(8,128)(2,1)S(1)} %get-tuple-element.13), channel_id=1, source_target_pairs={{0,2},{2,4},{4,6},{6,0},{1,3},{3,5},{5,7},{7,1},{8,10},{10,12},{12... | collective-permute-start | bytes 393224 | tf_op jit(solution)/shard_map/ppermute | solution.py:251
  30.9 3.6 %collective-permute-start.2 = (bf16[64,1024]{1,0:T(8,128)(2,1)S(1)}, bf16[64,1024]{1,0:T(8,128)(2,1)S(1)}, u32[]{:S(2)}, u32[]{:S(2)}) collective-permute-start(bf16[64,1024]{1,0:T(8,128)(2,1)S(1)} %get-tuple-element.14), channel_id=1, source_target_pairs={{0,6},{2,0},{4,2},{6,4},{1,7},{3,1},{5,3},{7,5},{8,14},{10,8},{12,... | collective-permute-start | bytes 393224 | tf_op jit(solution)/shard_map/ppermute | solution.py:251
  34.5 0.0 copy-start
  34.5 3.9 %collective-permute-start.4 = (bf16[64,1024]{1,0:T(8,128)(2,1)S(1)}, bf16[64,1024]{1,0:T(8,128)(2,1)S(1)}, u32[]{:S(2)}, u32[]{:S(2)}) collective-permute-start(bf16[64,1024]{1,0:T(8,128)(2,1)S(1)} %get-tuple-element.16), channel_id=1, source_target_pairs={{0,4},{2,6},{4,0},{6,2},{1,5},{3,7},{5,1},{7,3},{8,12},{10,14},{12... | collective-permute-start | bytes 393224 | tf_op jit(solution)/shard_map/ppermute | solution.py:251
  38.4 0.0 copy-done
  38.4 0.1 select_reduce_fusion
  38.5 0.6 slice.3
  41.6 0.1 copy.10.begin_ref
  41.8 3.6 %collective-permute-done.4.refs_1_ = bf16[64,1024]{1,0:T(8,128)(2,1)S(1)} collective-permute-done((bf16[64,1024]{1,0:T(8,128)(2,1)S(1)}, bf16[64,1024]{1,0:T(8,128)(2,1)S(1)}, u32[]{:S(2)}, u32[]{:S(2)}) %collective-permute-start.4) | collective-permute-done | bytes 131104 | tf_op jit(solution)/shard_map/ppermute | solution.py:251
  45.3 0.0 all-to-all-done
  45.3 2.5 %attend.2.refs_3_ = bf16[128,1024]{1,0:T(8,128)(2,1)S(1)} custom-call(s32[1]{0:T(128)S(6)} %min.3.need_ref, s32[256,1]{1,0:T(8,128)S(1)} %copy.10.begin_ref, bf16[64,1024]{1,0:T(8,128)(2,1)S(1)} %get-tuple-element.15.refs_0_, bf16[64,1024]{1,0:T(8,128)(2,1)S(1)} %collective-permute-done.4.refs_1_, bf16[64,2,32,128]{3,2,1,0:T(8,128)(2,1)S(1)} %bitcast.12), custom_call_target="tpu_custom_call" | custom-call | tf_op jit(solution)/shard_map/attend/pallas_call | solution.py:221
  47.8 0.0 collective-permute-done.1.refs_0_
  47.8 0.0 collective-permute-done.2.refs_1_
  47.8 2.7 %attend.3 = bf16[256,1024]{1,0:T(8,128)(2,1)S(1)} custom-call(s32[1]{0:T(128)S(6)} %min.3.need_ref, s32[256,1]{1,0:T(8,128)S(1)} %copy.10.begin_ref, bf16[64,1024]{1,0:T(8,128)(2,1)S(1)} %collective-permute-done.1.refs_0_, bf16[64,1024]{1,0:T(8,128)(2,1)S(1)} %collective-permute-done.2.refs_1_, bf16[64,2,32,128]{3,2,1,0:T(8,128)(2,1)S(1)} %bitcast.13, ...), custom_call_target="tpu_custom_call" | custom-call | tf_op jit(solution)/shard_map/attend/pallas_call | solution.py:221
  50.5 12.8 %all_to_all.20 = bf16[8,32,1024]{2,1,0:T(8,128)(2,1)S(1)} all-to-all(bf16[8,32,1024]{2,1,0:T(8,128)(2,1)S(1)} %bitcast.14), channel_id=1, replica_groups=mesh['z'=16,'odd'=2,'x'=4,'y'=4,'core'=2] {'y','core'}, dimensions={0} | all-to-all | bytes 1048576 | tf_op jit(solution)/shard_map/all_to_all | solution.py:260
  63.3 0.8 %copy.12 = bf16[4,8,8,1024]{3,1,2,0:T(8,128)(2,1)} copy(bf16[4,8,8,1024]{3,1,0,2:T(8,128)(2,1)S(1)} %bitcast.15) | data formatting | bytes 1048576
  (2 shorter events, 0.0 us)
Async XLA Ops:
  0.9 11.9 %collective-permute-start.3 = (bf16[64,1024]{1,0:T(8,128)(2,1)S(1)}, bf16[64,1024]{1,0:T(8,128)(2,1)S(1)}, u32[]{:S(2)}, u32[]{:S(2)}) collective-permute-start(bf16[64,1024]{1,0:T(8,128)(2,1)S(1)} %join.1.own_ref), channel_id=1, source_target_pairs={{0,64},{64,128},{128,192},{192,256},{256,320},{320,384},{384,448},... | collective-permute-start | bytes 393224 | tf_op jit(solution)/shard_map/ppermute | solution.py:242
  14.0 31.3 %all-to-all-start = ((bf16[64,64,128]{2,1,0:T(8,128)(2,1)}), bf16[64,64,128]{2,1,0:T(8,128)(2,1)S(1)}, u32[]{:S(2)}, u32[]{:S(2)}) async-start(bf16[64,64,128]{2,1,0:T(8,128)(2,1)} %pack.1), calls=%async_computation | async-start | bytes 2097152 | tf_op jit(solution)/shard_map/all_to_all | solution.py:244
  24.0 3.4 %collective-permute-start = (bf16[4,32,1024]{2,1,0:T(8,128)(2,1)S(1)}, bf16[4,32,1024]{2,1,0:T(8,128)(2,1)S(1)}, u32[]{:S(2)}, u32[]{:S(2)}) collective-permute-start(bf16[4,32,1024]{2,1,0:T(8,128)(2,1)S(1)} %get-tuple-element.12), channel_id=1, source_target_pairs={{0,1},{1,0},{2,3},{3,2},{4,5},{5,4},{6,7},{7,6},{8,9},{9,8},{10,11... | collective-permute-start | bytes 786440 | tf_op jit(solution)/shard_map/ppermute | solution.py:247
  27.5 20.4 %collective-permute-start.1 = (bf16[64,1024]{1,0:T(8,128)(2,1)S(1)}, bf16[64,1024]{1,0:T(8,128)(2,1)S(1)}, u32[]{:S(2)}, u32[]{:S(2)}) collective-permute-start(bf16[64,1024]{1,0:T(8,128)(2,1)S(1)} %get-tuple-element.13), channel_id=1, source_target_pairs={{0,2},{2,4},{4,6},{6,0},{1,3},{3,5},{5,7},{7,1},{8,10},{10,12},{12... | collective-permute-start | bytes 393224 | tf_op jit(solution)/shard_map/ppermute | solution.py:251
  30.9 16.9 %collective-permute-start.2 = (bf16[64,1024]{1,0:T(8,128)(2,1)S(1)}, bf16[64,1024]{1,0:T(8,128)(2,1)S(1)}, u32[]{:S(2)}, u32[]{:S(2)}) collective-permute-start(bf16[64,1024]{1,0:T(8,128)(2,1)S(1)} %get-tuple-element.14), channel_id=1, source_target_pairs={{0,6},{2,0},{4,2},{6,4},{1,7},{3,1},{5,3},{7,5},{8,14},{10,8},{12,... | collective-permute-start | bytes 393224 | tf_op jit(solution)/shard_map/ppermute | solution.py:251
  34.5 3.9 %copy-start = (s32[77]{0:T(128)S(1)}, s32[77]{0:T(128)}, u32[]{:S(2)}) copy-start(s32[77]{0:T(128)} %param.7) | copy-start | bytes 928
  34.5 10.8 %collective-permute-start.4 = (bf16[64,1024]{1,0:T(8,128)(2,1)S(1)}, bf16[64,1024]{1,0:T(8,128)(2,1)S(1)}, u32[]{:S(2)}, u32[]{:S(2)}) collective-permute-start(bf16[64,1024]{1,0:T(8,128)(2,1)S(1)} %get-tuple-element.16), channel_id=1, source_target_pairs={{0,4},{2,6},{4,0},{6,2},{1,5},{3,7},{5,1},{7,3},{8,12},{10,14},{12... | collective-permute-start | bytes 393224 | tf_op jit(solution)/shard_map/ppermute | solution.py:251
